TPU v7x, 32 devices: a whole 2x2x4 slice. The times are simulated.
32 devices in a mesh: blk: 8 (over y, x, core), grp: 4 (over z).
Axes of the slice: x: 2, y: 2, z: 4, core: 2. Of those that a mesh axis runs over, the one named last changes fastest.
Arguments:
- samples: float32 [32, 128, 256], P('blk', 'grp'), may hold values from -11 to 11
- pair_table: int32 [32, 16], P('blk'), may hold values from 0 to 31
- assignment: int32 [2, 32], P(None, 'blk'), may hold values from 0 to 127
- band_index: int32 [2], replicated, may hold values from 0 to 1023
Outputs:
- log_weight: float32 [2, 32, 128], P(None, 'blk', 'grp')
All inputs are finite; a program needn't handle non-finite values.
Results may differ from a plain program's by a relative error of at most 0.0003.
Values sent between devices are 32-bit elements; how exact they have to be, the bound alone decides.
No kernel may reach another device: no remote copies, remote signals or barrier semaphores. Data moves between devices by JAX's collectives and lax.ppermute only.
A program may use at most 128 MiB of HBM per device.

v0:
```python
import jax
import jax.numpy as jnp
from jax import lax
from jax.sharding import PartitionSpec as P

PAIRS = 16


def joined_2(shard, axis, combine):
    everything = jax.tree.map(lambda part: lax.all_gather(part, axis), shard)
    initial = jax.tree.map(lambda part: part[0], everything)

    def hop(k, so_far):
        return combine(so_far, jax.tree.map(lambda part: part[k], everything))

    return lax.fori_loop(1, lax.axis_size(axis), hop, initial)


def make_fold(queries, query_norm, band_list, counts):

    def fold(state, shard_rows, offset):
        count_in = shard_rows.shape[0]
        rows_dev = shard_rows.shape[1]

        def compute(inner):
            key_rows = shard_rows.reshape(count_in * rows_dev, shard_rows.shape[2])
            key_norm = jnp.sum(key_rows * key_rows, -1)
            product = jnp.einsum("qd,kd->qk", queries, key_rows, precision=lax.Precision.HIGHEST)
            distance = query_norm[:, None] + key_norm[None, :] - 2.0 * product
            blocks = []
            for band_sq in band_list:
                scores = (-distance / (2.0 * band_sq)).reshape(
                    distance.shape[0], count_in, rows_dev
                )
                peak = jnp.max(scores, -1)
                blocks.append(peak + jnp.log(jnp.sum(jnp.exp(scores - peak[..., None]), -1)))
            update = jnp.stack(blocks)
            return lax.dynamic_update_slice(inner, update, (0, 0, offset))

        needed = jnp.any(counts > 0)
        return lax.cond(needed, compute, lambda inner: inner, state)

    return fold


def per_device(samples, pair_table, assignment, band_index):
    local_subs, rows_dev, width = samples.shape
    rounds = assignment.shape[0]
    group_size = lax.axis_size("grp")
    group_index = lax.axis_index("grp")
    members = local_subs * lax.axis_size("blk")
    band_sq = width * (1.0 + band_index.astype(jnp.float32) / 256.0) / 32.0
    local_pick = assignment - group_index * rows_dev
    onehot = (
        local_pick[:, :, None] == jnp.arange(rows_dev, dtype=jnp.int32)[None, None, :]
    ).astype(jnp.float32)
    picked = jnp.einsum("tsr,srd->td", onehot, samples, precision=lax.Precision.HIGHEST)
    centre = lax.psum(picked, ("blk", "grp")) / members
    member_ids = jnp.arange(members, dtype=jnp.int32)
    count_int = jnp.sum(
        (pair_table[:, :, None] == member_ids[None, None, :]).astype(jnp.int32), axis=1
    )
    counts = count_int.astype(jnp.float32)
    gathered = lax.all_gather(samples, "grp", axis=1, tiled=True)
    query_count = local_subs * rows_dev * group_size
    queries = gathered.reshape(query_count, width)
    query_norm = jnp.sum(queries * queries, -1)
    start_state = jnp.zeros((rounds, query_count, members), jnp.float32)
    fold = make_fold(queries, query_norm, [band_sq[turn] for turn in range(rounds)], count_int)
    partial_value = fold(
        start_state, lax.all_gather(samples, "blk", axis=0, tiled=True), jnp.int32(0)
    )
    split_view = partial_value.reshape(rounds, local_subs, group_size, rows_dev, members)
    swapped = lax.all_to_all(split_view, "grp", split_axis=2, concat_axis=2, tiled=True)
    peak = jnp.max(swapped, 2)
    kernel = peak + jnp.log(jnp.sum(jnp.exp(swapped - peak[:, :, None]), 2))
    weighted = jnp.einsum("tsrm,sm->tsr", kernel, counts, precision=lax.Precision.HIGHEST) / PAIRS
    spread = samples[None] - centre[:, None, None, :]
    logits = weighted - jnp.sum(spread * spread, -1) / (2.0 * band_sq[:, None, None])
    row_peak = jnp.max(logits, -1)
    row_total = jnp.sum(jnp.exp(logits - row_peak[..., None]), -1)

    def combine_pair(first, second):
        joined = jnp.maximum(first[0], second[0])
        return (
            joined,
            first[1] * jnp.exp(first[0] - joined) + second[1] * jnp.exp(second[0] - joined),
        )

    peak_all, total_all = joined_2((row_peak, row_total), "grp", combine_pair)
    return logits - peak_all[..., None] - jnp.log(total_all)[..., None]


def solution(mesh):
    return jax.shard_map(
        per_device,
        mesh=mesh,
        in_specs=(P("blk", "grp", None), P("blk", None), P(None, "blk"), P()),
        out_specs=P(None, "blk", "grp"),
        check_vma=False,
    )
```

profile of v0, /device:TPU:0, one launch (start us, length us, event | category | flops | bytes accessed | tf_op | source)
XLA Modules:
  0.0 123.1 jit_solution(9642932200936565193)
XLA Ops:
  6.5 0.0 all-gather.6.cloned.1.call-start
  6.5 0.7 all-gather.6.cloned.1.call-update
  7.3 0.8 convert_reduce_fusion
  8.0 0.6 compare_reduce_fusion
  9.3 0.7 broadcast_subtract_fusion
  10.0 0.1 copy.19
  10.1 1.2 convolution_bitcast_fusion
  11.3 42.0 %psum.7 = f32[2,256]{1,0:T(2,128)S(1)} all-reduce(f32[2,256]{1,0:T(2,128)S(1)} %convolution_bitcast_fusion), channel_id=1, replica_groups=mesh['blk'=8,'grp'=4] {'blk','grp'}, use_global_device_ids=true, to_apply=%region_12.0 | all-reduce | flops 512 | bytes 4096 | tf_op jit(solution)/shard_map/psum | solution.py:58
  53.2 15.9 %all_gather.18 = f32[4,128,256]{2,1,0:T(8,128)S(1)} all-gather(f32[4,32,256]{2,1,0:T(8,128)} %param.8), channel_id=1, replica_groups=mesh['blk'=8,'grp'=4] {'grp'}, dimensions={1}, use_global_device_ids=true | all-gather | bytes 655360 | tf_op jit(solution)/shard_map/all_gather | solution.py:64
  69.2 0.7 multiply_add_fusion
  69.8 0.0 all-gather.6.cloned.1.call-done
  69.8 14.7 %conditional.1 = (f32[2,512,32]{1,2,0:T(8,128)S(1)}) conditional(s32[]{:T(128)} %convert_element_type.15, () %tuple.36, (f32[4,128,256]{2,1,0:T(8,128)S(1)}, f32[32,32,256]{2,1,0:T(8,128)}, f32[2]{0:T(128)S(1)}) %tuple.37), branch_computations={%region_2.0_spmd, %region_3.10_spmd} | conditional | flops 1617689088 | bytes 25186376 | solution.py:41
  69.8 1.4 %multiply_reduce_fusion = f32[32,32]{1,0:T(8,128)S(1)} fusion(f32[32,32,256]{2,1,0:T(8,128)} %get-tuple-element.164), kind=kLoop, calls=%fused_computation.11 | loop fusion | flops 523264 | bytes 1052672 | tf_op jit(solution)/shard_map/cond/branch_1_fun/reduce_sum | solution.py:27
  71.3 0.1 add.87
  71.3 0.7 fusion.12
  73.4 0.1 multiply_reduce_fusion.1
  73.5 5.3 %broadcast_divide_fusion.1 = (f32[512,1024]{1,0:T(8,128)}, f32[512,1024]{1,0:T(8,128)}) fusion(f32[]{:T(128)} %bitcast.3, f32[]{:T(128)} %bitcast.6, f32[512,256]{1,0:T(8,128)S(1)} %bitcast.71, f32[1024,256]{1,0:T(8,128)} %bitcast.74, f32[1024]{0:T(1024)S(1)} %add.87, f32[512]{0:T(512)S(1)} %bitcast.80), kind=kOutput, calls=%fused_computation.10 | convolution fusion | flops 1613758464 | bytes 5773320 | tf_op jit(solution)/shard_map/cond/branch_1_fun/qd,kd->qk/dot_general | solution.py:28
  78.8 1.9 %copy.16 = f32[512,1024]{0,1:T(8,128)S(1)} copy(f32[512,1024]{1,0:T(8,128)} %get-tuple-element.190) | data formatting | bytes 4194304 | tf_op jit(solution)/shard_map/cond/branch_1_fun/div | solution.py:32
  80.8 0.3 bitcast_reduce_fusion.1
  81.1 0.5 fusion.3
  81.6 1.9 %copy.17 = f32[512,1024]{0,1:T(8,128)S(1)} copy(f32[512,1024]{1,0:T(8,128)} %get-tuple-element.191) | data formatting | bytes 4194304 | tf_op jit(solution)/shard_map/cond/branch_1_fun/div | solution.py:32
  83.6 0.3 bitcast_reduce_fusion
  83.9 0.5 fusion.1
  84.5 0.0 copy-start
  84.5 0.3 reshape.79
  84.8 0.1 copy.28
  84.9 1.0 reshape.97
  85.9 3.8 %all-to-all-start = ((f32[4,1,8192]{2,1,0:T(1,128)}), f32[4,1,8192]{2,1,0:T(1,128)S(1)}, u32[]{:S(2)}, u32[]{:S(2)}) async-start(f32[4,1,8192]{2,1,0:T(1,128)} %reshape.97), calls=%async_computation | async-start | bytes 262144 | tf_op jit(solution)/shard_map/all_to_all | solution.py:74
  89.7 0.0 copy-done
  89.7 0.1 multiply_reduce_fusion.2
  89.8 5.8 %all-to-all-done = f32[4,1,8192]{2,1,0:T(1,128)S(1)} async-done(((f32[4,1,8192]{2,1,0:T(1,128)}), f32[4,1,8192]{2,1,0:T(1,128)S(1)}, u32[]{:S(2)}, u32[]{:S(2)}) %all-to-all-start) | async-done | bytes 131104 | tf_op jit(solution)/shard_map/all_to_all | solution.py:74
  95.6 0.5 broadcast.44
  96.1 1.0 reduce.5
  97.1 0.3 reshape.98
  97.4 0.1 bitcast_reduce_fusion.2
  97.6 0.2 exponential_reduce_fusion
  97.8 0.2 fusion.6
  98.0 0.2 fusion.11
  98.2 0.2 exponential_reduce_fusion.1
  98.3 9.0 %all-gather.3 = f32[4,2,4]{2,1,0:T(2,128)S(1)} all-gather(f32[1,2,4]{2,1,0:T(2,128)S(1)} %bitcast.79), channel_id=3, replica_groups=mesh['blk'=8,'grp'=4] {'grp'}, dimensions={0}, use_global_device_ids=true | all-gather | bytes 160 | tf_op jit(solution)/shard_map/all_gather | solution.py:10
  107.3 8.2 %all-gather.2 = f32[4,2,4]{2,1,0:T(2,128)S(1)} all-gather(f32[1,2,4]{2,1,0:T(2,128)S(1)} %bitcast.77), channel_id=2, replica_groups=mesh['blk'=8,'grp'=4] {'grp'}, dimensions={0}, use_global_device_ids=true | all-gather | bytes 160 | tf_op jit(solution)/shard_map/all_gather | solution.py:10
  115.5 0.1 while.17
  115.6 0.7 subtract_subtract_fusion
  (12 shorter events, 0.2 us)
Async XLA Ops:
  6.5 63.3 %all-gather.6.cloned.1.call-start = ((), (), s32[]{:S(2)}) async-start(), calls=%async_computation.1 | async-start | bytes 1179648 | tf_op jit(solution)/shard_map/all_gather | solution.py:71
  84.5 5.2 %copy-start = (f32[4,32,256]{2,1,0:T(8,128)S(1)}, f32[4,32,256]{2,1,0:T(8,128)}, u32[]{:S(2)}) copy-start(f32[4,32,256]{2,1,0:T(8,128)} %param.8) | copy-start | bytes 393220
  85.9 9.7 %all-to-all-start = ((f32[4,1,8192]{2,1,0:T(1,128)}), f32[4,1,8192]{2,1,0:T(1,128)S(1)}, u32[]{:S(2)}, u32[]{:S(2)}) async-start(f32[4,1,8192]{2,1,0:T(1,128)} %reshape.97), calls=%async_computation | async-start | bytes 262144 | tf_op jit(solution)/shard_map/all_to_all | solution.py:74
Sparse Core Ops, SparseCore 0:
  9.2 26.2 all-gather.5
where the time goes:
time: 124 us; the launch traced here: 123 us
  blocking collectives  75 us (60%)
  between operations  14.1 us (11%)
  other arithmetic  8.66 us (7%)
  local copies, waits for them, and re-layouts  6.86 us (6%)
  matrix products  6.7 us (5%)
  waiting for transfers between devices  6.5 us (5%)
  starting transfers between devices  3.8 us (3%)
  loops' own time  1.43 us (1%)
    psum x1, blocking collectives, per_device(): centre = lax.psum(picked, ('blk', 'grp')) / members  42 us
    all_gather x2, blocking collectives, joined_2(): everything = jax.tree.map(lambda part: lax.all_gather(part, axis), shard)  17.2 us
    all_gather x1, blocking collectives, per_device(): gathered = lax.all_gather(samples, 'grp', axis=1, tiled=True)  15.9 us
    all_to_all x1, waiting for transfers between devices, per_device(): lax.all_to_all(split_view, 'grp', split_axis=2, concat_axis=2, tiled=True)  5.79 us
    dot_general x1, matrix products, compute(): jnp.einsum('qd,kd->qk', queries, key_rows, precision=lax.Precision.HIGHEST)  5.35 us
    div x2, local copies, waits for them, and re-layouts, compute(): -distance / (2.0 * band_sq)  3.84 us
    all_to_all x1, starting transfers between devices, per_device(): lax.all_to_all(split_view, 'grp', split_axis=2, concat_axis=2, tiled=True)  3.8 us
  transfers between devices with their start and end apart: 2, of which 1 were waited for; matrix products, arithmetic and copies ran while one was open for 3% of the time, Pallas kernels for 0%

commit v1 on v0

--- a/solution.py
+++ b/solution.py
@@ -55,7 +55,7 @@
         local_pick[:, :, None] == jnp.arange(rows_dev, dtype=jnp.int32)[None, None, :]
     ).astype(jnp.float32)
     picked = jnp.einsum("tsr,srd->td", onehot, samples, precision=lax.Precision.HIGHEST)
-    centre = lax.psum(picked, ("blk", "grp")) / members
+    centre = lax.psum(lax.psum(picked, "grp"), "blk") / members
     member_ids = jnp.arange(members, dtype=jnp.int32)
     count_int = jnp.sum(
         (pair_table[:, :, None] == member_ids[None, None, :]).astype(jnp.int32), axis=1

time: 124 us -> 107 us (0.86)
  blocking collectives: 75 us -> 58.9 us
    psum x1 -> x2, blocking collectives: 42 us -> 25.4 us  [per_device(): centre = lax.psum(lax.psum(picked, 'grp'), 'blk') / members]
  transfers between devices with their start and end apart: 2 -> 2, of which waited for: 1 -> 1; matrix products, arithmetic and copies ran while one was open for 3% -> 4% of each run, Pallas kernels for 0% -> 0%
where the time goes in v1:
time: 107 us; the launch traced here: 106 us
  blocking collectives  58.9 us (55%)
  between operations  14.2 us (13%)
  other arithmetic  8.66 us (8%)
  local copies, waits for them, and re-layouts  6.86 us (6%)
  matrix products  6.7 us (6%)
  waiting for transfers between devices  6.45 us (6%)
  starting transfers between devices  3.32 us (3%)
  loops' own time  1.43 us (1%)
    psum x2, blocking collectives, per_device(): centre = lax.psum(lax.psum(picked, 'grp'), 'blk') / members  25.4 us
    all_gather x2, blocking collectives, joined_2(): everything = jax.tree.map(lambda part: lax.all_gather(part, axis), shard)  17.2 us
    all_gather x1, blocking collectives, per_device(): gathered = lax.all_gather(samples, 'grp', axis=1, tiled=True)  16.3 us
    all_to_all x1, waiting for transfers between devices, per_device(): lax.all_to_all(split_view, 'grp', split_axis=2, concat_axis=2, tiled=True)  5.73 us
    dot_general x1, matrix products, compute(): jnp.einsum('qd,kd->qk', queries, key_rows, precision=lax.Precision.HIGHEST)  5.35 us
    div x2, local copies, waits for them, and re-layouts, compute(): -distance / (2.0 * band_sq)  3.84 us
    all_to_all x1, starting transfers between devices, per_device(): lax.all_to_all(split_view, 'grp', split_axis=2, concat_axis=2, tiled=True)  3.32 us
  transfers between devices with their start and end apart: 2, of which 1 were waited for; matrix products, arithmetic and copies ran while one was open for 4% of the time, Pallas kernels for 0%

profile of v1, /device:TPU:0, one launch (start us, length us, event | category | flops | bytes accessed | tf_op | source)
XLA Modules:
  0.0 106.5 jit_solution(3748019330601630338)
XLA Ops:
  6.5 0.0 all-gather.6.cloned.1.call-start
  6.5 0.7 all-gather.6.cloned.1.call-update
  7.3 0.8 convert_reduce_fusion
  8.0 0.6 compare_reduce_fusion
  9.3 0.7 broadcast_subtract_fusion
  10.0 0.1 copy.19
  10.1 1.2 %convolution_bitcast_fusion = f32[2,256]{1,0:T(2,128)S(1)} fusion(f32[4,32,256]{2,1,0:T(8,128)} %param.8, s32[2,4]{0,1:T(4,128)S(1)} %copy.19), kind=kOutput, calls=%fused_computation.22 | convolution fusion | flops 786688 | bytes 133152 | tf_op jit(solution)/shard_map/tsr,srd->td/dot_general | solution.py:57
  11.3 13.5 %psum.14 = f32[2,256]{1,0:T(2,128)S(1)} all-reduce(f32[2,256]{1,0:T(2,128)S(1)} %convolution_bitcast_fusion), channel_id=1, replica_groups=mesh['blk'=8,'grp'=4] {'grp'}, use_global_device_ids=true, to_apply=%region_12.0 | all-reduce | flops 512 | bytes 4096 | tf_op jit(solution)/shard_map/psum | solution.py:58
  24.7 11.9 %psum.15 = f32[2,256]{1,0:T(2,128)S(1)} all-reduce(f32[2,256]{1,0:T(2,128)S(1)} %psum.14), channel_id=1, replica_groups=mesh['blk'=8,'grp'=4] {'blk'}, use_global_device_ids=true, to_apply=%region_13.0 | all-reduce | flops 512 | bytes 4096 | tf_op jit(solution)/shard_map/psum | solution.py:58
  36.7 16.3 %all_gather.18 = f32[4,128,256]{2,1,0:T(8,128)S(1)} all-gather(f32[4,32,256]{2,1,0:T(8,128)} %param.8), channel_id=1, replica_groups=mesh['blk'=8,'grp'=4] {'grp'}, dimensions={1}, use_global_device_ids=true | all-gather | bytes 655360 | tf_op jit(solution)/shard_map/all_gather | solution.py:64
  53.0 0.7 multiply_add_fusion
  53.7 0.0 all-gather.6.cloned.1.call-done
  53.7 14.7 %conditional.1 = (f32[2,512,32]{1,2,0:T(8,128)S(1)}) conditional(s32[]{:T(128)} %convert_element_type.15, () %tuple.36, (f32[4,128,256]{2,1,0:T(8,128)S(1)}, f32[32,32,256]{2,1,0:T(8,128)}, f32[2]{0:T(128)S(1)}) %tuple.37), branch_computations={%region_2.0_spmd, %region_3.10_spmd} | conditional | flops 1617689088 | bytes 25186376 | solution.py:41
  53.7 1.4 %multiply_reduce_fusion = f32[32,32]{1,0:T(8,128)S(1)} fusion(f32[32,32,256]{2,1,0:T(8,128)} %get-tuple-element.164), kind=kLoop, calls=%fused_computation.11 | loop fusion | flops 523264 | bytes 1052672 | tf_op jit(solution)/shard_map/cond/branch_1_fun/reduce_sum | solution.py:27
  55.1 0.1 add.89
  55.2 0.7 fusion.12
  57.2 0.1 multiply_reduce_fusion.1
  57.4 5.3 %broadcast_divide_fusion.1 = (f32[512,1024]{1,0:T(8,128)}, f32[512,1024]{1,0:T(8,128)}) fusion(f32[]{:T(128)} %bitcast.3, f32[]{:T(128)} %bitcast.6, f32[512,256]{1,0:T(8,128)S(1)} %bitcast.71, f32[1024,256]{1,0:T(8,128)} %bitcast.74, f32[1024]{0:T(1024)S(1)} %add.89, f32[512]{0:T(512)S(1)} %bitcast.80), kind=kOutput, calls=%fused_computation.10 | convolution fusion | flops 1613758464 | bytes 5773320 | tf_op jit(solution)/shard_map/cond/branch_1_fun/qd,kd->qk/dot_general | solution.py:28
  62.7 1.9 %copy.16 = f32[512,1024]{0,1:T(8,128)S(1)} copy(f32[512,1024]{1,0:T(8,128)} %get-tuple-element.190) | data formatting | bytes 4194304 | tf_op jit(solution)/shard_map/cond/branch_1_fun/div | solution.py:32
  64.6 0.3 bitcast_reduce_fusion.1
  65.0 0.5 fusion.3
  65.5 1.9 %copy.17 = f32[512,1024]{0,1:T(8,128)S(1)} copy(f32[512,1024]{1,0:T(8,128)} %get-tuple-element.191) | data formatting | bytes 4194304 | tf_op jit(solution)/shard_map/cond/branch_1_fun/div | solution.py:32
  67.4 0.3 bitcast_reduce_fusion
  67.8 0.5 fusion.1
  68.4 0.0 copy-start
  68.4 0.3 reshape.79
  68.6 0.1 copy.28
  68.8 1.0 reshape.97
  69.8 3.3 %all-to-all-start = ((f32[4,1,8192]{2,1,0:T(1,128)}), f32[4,1,8192]{2,1,0:T(1,128)S(1)}, u32[]{:S(2)}, u32[]{:S(2)}) async-start(f32[4,1,8192]{2,1,0:T(1,128)} %reshape.97), calls=%async_computation | async-start | bytes 262144 | tf_op jit(solution)/shard_map/all_to_all | solution.py:74
  73.1 0.0 copy-done
  73.1 0.1 multiply_reduce_fusion.2
  73.2 5.7 %all-to-all-done = f32[4,1,8192]{2,1,0:T(1,128)S(1)} async-done(((f32[4,1,8192]{2,1,0:T(1,128)}), f32[4,1,8192]{2,1,0:T(1,128)S(1)}, u32[]{:S(2)}, u32[]{:S(2)}) %all-to-all-start) | async-done | bytes 131104 | tf_op jit(solution)/shard_map/all_to_all | solution.py:74
  79.0 0.5 broadcast.44
  79.5 1.0 reduce.5
  80.5 0.3 reshape.98
  80.8 0.1 bitcast_reduce_fusion.2
  80.9 0.2 exponential_reduce_fusion
  81.2 0.2 fusion.6
  81.4 0.2 fusion.11
  81.5 0.2 exponential_reduce_fusion.1
  81.7 9.0 %all-gather.3 = f32[4,2,4]{2,1,0:T(2,128)S(1)} all-gather(f32[1,2,4]{2,1,0:T(2,128)S(1)} %bitcast.79), channel_id=3, replica_groups=mesh['blk'=8,'grp'=4] {'grp'}, dimensions={0}, use_global_device_ids=true | all-gather | bytes 160 | tf_op jit(solution)/shard_map/all_gather | solution.py:10
  90.7 8.2 %all-gather.2 = f32[4,2,4]{2,1,0:T(2,128)S(1)} all-gather(f32[1,2,4]{2,1,0:T(2,128)S(1)} %bitcast.77), channel_id=2, replica_groups=mesh['blk'=8,'grp'=4] {'grp'}, dimensions={0}, use_global_device_ids=true | all-gather | bytes 160 | tf_op jit(solution)/shard_map/all_gather | solution.py:10
  98.9 0.1 while.17
  99.0 0.7 subtract_subtract_fusion
  (12 shorter events, 0.2 us)
Async XLA Ops:
  6.5 47.1 %all-gather.6.cloned.1.call-start = ((), (), s32[]{:S(2)}) async-start(), calls=%async_computation.1 | async-start | bytes 1179648 | tf_op jit(solution)/shard_map/all_gather | solution.py:71
  68.4 4.8 %copy-start = (f32[4,32,256]{2,1,0:T(8,128)S(1)}, f32[4,32,256]{2,1,0:T(8,128)}, u32[]{:S(2)}) copy-start(f32[4,32,256]{2,1,0:T(8,128)} %param.8) | copy-start | bytes 393220
  69.8 9.2 %all-to-all-start = ((f32[4,1,8192]{2,1,0:T(1,128)}), f32[4,1,8192]{2,1,0:T(1,128)S(1)}, u32[]{:S(2)}, u32[]{:S(2)}) async-start(f32[4,1,8192]{2,1,0:T(1,128)} %reshape.97), calls=%async_computation | async-start | bytes 262144 | tf_op jit(solution)/shard_map/all_to_all | solution.py:74
Sparse Core Ops, SparseCore 0:
  9.2 26.1 all-gather.5
